TPU v7x, 128 devices: a whole 4x4x4 slice. The times are simulated.
128 devices in a mesh: row: 16 (over z_hi, x, core), col: 8 (over y, z_lo).
Axes of the slice: x: 4, y: 4, z: 4 (z_hi: 2, z_lo: 2; z = z_hi * 2 + z_lo), core: 2. Of those that a mesh axis runs over, the one named last changes fastest.
Arguments:
- pair: bfloat16 [512, 512, 128], P('row', 'col'), may hold values from -6 to 6
- cotangent: bfloat16 [512, 512, 128], P('row', 'col'), may hold values from -6 to 6
- length: int32 [1], replicated, may hold values from 256 to 512
- norm_gain: float32 [128], replicated, may hold values from 0.1 to 1.9
- norm_bias: float32 [128], replicated, may hold values from -1.5 to 1.5
- left_weight: bfloat16 [128, 256], replicated, may hold values from -0.5 to 0.5
- right_weight: bfloat16 [128, 256], replicated, may hold values from -0.5 to 0.5
- gate_weight: bfloat16 [128, 128], replicated, may hold values from -0.5 to 0.5
- out_gain: float32 [128], replicated, may hold values from 0.1 to 1.9
- out_bias: float32 [128], replicated, may hold values from -2 to 2
- out_weight: bfloat16 [128, 128], replicated, may hold values from -0.5 to 0.5
Outputs:
- update: bfloat16 [512, 512, 128], P('row', 'col')
- grad_pair: bfloat16 [512, 512, 128], P('row', 'col')
- grad_left: float32 [128, 256], replicated
- grad_right: float32 [128, 256], replicated
- grad_gating: float32 [128, 128], replicated
- grad_output: float32 [128, 128], replicated
- grad_norms: float32 [4, 128], replicated
Inputs may be any that keep to these rules, and one draw needn't show every extreme that they name: Tokens at positions 511 down to length are padding.
All inputs are finite; a program needn't handle non-finite values.
Results may differ from a plain program's by a relative error of at most 0.014.
Values may be sent and summed in bfloat16 or wider, within the bound.
A program may use at most 128 MiB of HBM per device.

v0:
```python
import jax
import jax.numpy as jnp
from jax import lax
from jax.sharding import PartitionSpec as P

EPS = 1e-05


def broadcast(block, axis, holder):
    block = jnp.where(lax.axis_index(axis) == holder, block, jnp.zeros_like(block))
    return lax.psum(block, axis)


def split_up(x, dim, peers):
    dims = x.shape
    tiles = x.reshape(*dims[:dim], peers, dims[dim] // peers, *dims[dim + 1 :])
    return jnp.moveaxis(tiles, dim, 0)


def summed_on_arrival(x, axis, dim):
    peers = lax.axis_size(axis)
    tiles = lax.all_to_all(split_up(x, dim, peers), axis, 0, 0, tiled=True)
    return jnp.sum(tiles.astype(jnp.float32), axis=0)


def together(arrays, axis):
    flat, at, done = (jnp.concatenate([a.reshape(-1) for a in arrays]), 0, [])
    total = lax.psum(flat, axis)
    for a in arrays:
        done.append(total[at : at + a.size].reshape(a.shape))
        at += a.size
    return tuple(done)


def normalize(values):
    center = values - jnp.mean(values, axis=-1, keepdims=True)
    inverse = lax.rsqrt(jnp.mean(center * center, axis=-1, keepdims=True) + EPS)
    return (center * inverse, inverse)


def gating(panel, weight, first_ok, second_ok, hidden):
    projected = jnp.einsum("ikc,ch->ikh", panel, weight, preferred_element_type=jnp.float32)
    values = projected[..., :hidden]
    sigmoid_val = jax.nn.sigmoid(projected[..., hidden:])
    pad_mask = (first_ok[:, None] & second_ok[None, :]).astype(jnp.float32)[..., None]
    return ((pad_mask * sigmoid_val * values).astype(jnp.bfloat16), values, sigmoid_val, pad_mask)


def push_back(partial_value, values, sigmoid_val, pad_mask, weight, panel):
    combined = jnp.concatenate(
        [
            partial_value * pad_mask * sigmoid_val,
            partial_value * pad_mask * values * sigmoid_val * (1.0 - sigmoid_val),
        ],
        axis=-1,
    ).astype(jnp.bfloat16)
    panel_grad = jnp.einsum("ikh,ch->ikc", combined, weight, preferred_element_type=jnp.float32)
    weight_grad = jnp.einsum("ikc,ikh->ch", panel, combined, preferred_element_type=jnp.float32)
    return (panel_grad, weight_grad)


def per_device(
    pair,
    cotangent,
    length,
    norm_gain,
    norm_bias,
    left_weight,
    right_weight,
    gate_weight,
    out_gain,
    out_bias,
    out_weight,
):
    row_index = lax.axis_index("row")
    col_index = lax.axis_index("col")
    n_row = lax.axis_size("row")
    n_col = lax.axis_size("col")
    per_col = n_row // n_col
    rows_dev = pair.shape[0]
    cols_dev = pair.shape[1]
    tokens = rows_dev * n_row
    hidden = out_weight.shape[0]
    pair_hat, pair_scale = normalize(pair.astype(jnp.float32))
    normed = (pair_hat * norm_gain + norm_bias).astype(jnp.bfloat16)
    real_count = length[0]
    second_ok = jnp.arange(tokens, dtype=jnp.int32) < real_count
    own_ok = row_index * rows_dev + jnp.arange(rows_dev, dtype=jnp.int32) < real_count
    partner_ok = col_index * cols_dev + jnp.arange(cols_dev, dtype=jnp.int32) < real_count
    left_tile, left_val, left_sig, tile_mask = gating(
        normed, left_weight, own_ok, partner_ok, hidden
    )
    right_tile, right_val, right_sig, unused_mask = gating(
        normed, right_weight, own_ok, partner_ok, hidden
    )
    row_panel = lax.all_gather(normed, "col", axis=1, tiled=True)
    pieces = []
    for member in range(per_col):
        pieces.append(broadcast(row_panel, "row", col_index * per_col + member))
    col_panel = jnp.concatenate(pieces, axis=0)
    left_act = gating(row_panel, left_weight, own_ok, second_ok, hidden)[0]
    right_act = gating(col_panel, right_weight, partner_ok, second_ok, hidden)[0]
    tri = jnp.einsum("ikh,jkh->ijh", left_act, right_act, preferred_element_type=jnp.float32)
    tri_hat, tri_scale = normalize(tri)
    tri_normed = (tri_hat * out_gain + out_bias).astype(jnp.bfloat16)
    outer_val = jnp.einsum(
        "ijh,hc->ijc", tri_normed, out_weight, preferred_element_type=jnp.float32
    )
    gate_val = jax.nn.sigmoid(
        jnp.einsum("ijc,cd->ijd", normed, gate_weight, preferred_element_type=jnp.float32)
    )
    update = (gate_val * outer_val).astype(jnp.bfloat16)
    upstream = cotangent.astype(jnp.float32)
    outer_grad = (upstream * gate_val).astype(jnp.bfloat16)
    gate_grad = (upstream * outer_val * gate_val * (1.0 - gate_val)).astype(jnp.bfloat16)
    grad_output = jnp.einsum(
        "ijh,ijc->hc", tri_normed, outer_grad, preferred_element_type=jnp.float32
    )
    grad_gating = jnp.einsum("ijc,ijd->cd", normed, gate_grad, preferred_element_type=jnp.float32)
    tnorm_grad = jnp.einsum(
        "ijc,hc->ijh", outer_grad, out_weight, preferred_element_type=jnp.float32
    )
    hat_grad = tnorm_grad * out_gain
    tri_grad = (
        tri_scale
        * (
            hat_grad
            - jnp.mean(hat_grad, axis=-1, keepdims=True)
            - tri_hat * jnp.mean(hat_grad * tri_hat, axis=-1, keepdims=True)
        )
    ).astype(jnp.bfloat16)
    row_partial = jnp.einsum(
        "ijh,jkh->ikh", tri_grad, right_act, preferred_element_type=jnp.float32
    )
    col_partial = jnp.einsum("ijh,ikh->jkh", tri_grad, left_act, preferred_element_type=jnp.float32)
    row_part = summed_on_arrival(row_partial.astype(jnp.bfloat16), "col", 1)
    summed = lax.psum_scatter(
        col_partial.astype(jnp.bfloat16), "row", scatter_dimension=0, tiled=True
    )
    slab = summed[None]
    received = lax.all_to_all(slab, "col", split_axis=2, concat_axis=0, tiled=True)
    select = (jnp.arange(per_col, dtype=jnp.int32) == row_index // n_col).astype(jnp.bfloat16)
    spread = (received[:, None] * select[None, :, None, None, None]).reshape(
        (n_row,) + received.shape[1:]
    )
    returned = lax.all_to_all(spread, "row", split_axis=0, concat_axis=0, tiled=True)
    start = row_index % per_col * n_col
    owned = lax.dynamic_slice_in_dim(returned, start, n_col, 0).reshape(rows_dev, cols_dev, -1)
    col_part = owned.astype(jnp.float32)
    from_rows, grad_left = push_back(row_part, left_val, left_sig, tile_mask, left_weight, normed)
    from_cols, grad_right = push_back(
        col_part, right_val, right_sig, tile_mask, right_weight, normed
    )
    gate_back = jnp.einsum(
        "ijd,cd->ijc", gate_grad, gate_weight, preferred_element_type=jnp.float32
    )
    normed_grad = gate_back + from_rows + from_cols
    scaled = normed_grad * norm_gain
    grad_pair = (
        pair_scale
        * (
            scaled
            - jnp.mean(scaled, axis=-1, keepdims=True)
            - pair_hat * jnp.mean(scaled * pair_hat, axis=-1, keepdims=True)
        )
    ).astype(jnp.bfloat16)
    grad_norms = jnp.stack(
        [
            jnp.sum(normed_grad * pair_hat, axis=(0, 1)),
            jnp.sum(normed_grad, axis=(0, 1)),
            jnp.sum(tnorm_grad * tri_hat, axis=(0, 1)),
            jnp.sum(tnorm_grad, axis=(0, 1)),
        ]
    )
    totals = together((grad_left, grad_right, grad_gating, grad_output, grad_norms), ("row", "col"))
    inverse = 1.0 / tokens
    return (
        update,
        grad_pair,
        totals[0] * inverse,
        totals[1] * inverse,
        totals[2] * inverse,
        totals[3] * inverse,
        totals[4] * inverse,
    )


def solution(mesh):
    return jax.shard_map(
        per_device,
        mesh=mesh,
        in_specs=(
            P("row", "col", None),
            P("row", "col", None),
            P(),
            P(),
            P(),
            P(),
            P(),
            P(),
            P(),
            P(),
            P(),
        ),
        out_specs=(P("row", "col", None), P("row", "col", None), P(), P(), P(), P(), P()),
        check_vma=False,
    )
```

profile of v0, /device:TPU:1, one launch (start us, length us, event | category | flops | bytes accessed | tf_op | source)
XLA Modules:
  0.0 731.4 jit_solution(15539498948825562416)
XLA Ops:
  12.9 92.9 %all-gather.2.cloned.1.call-done = bf16[32,512,128]{2,1,0:T(8,128)(2,1)} async-done(((bf16[32,64,128]{2,1,0:T(8,128)(2,1)}), bf16[32,512,128]{2,1,0:T(8,128)(2,1)}) %all-gather.2.cloned.1.call-update) | async-done | bytes 4194320 | tf_op jit(solution)/shard_map/all_gather | solution.py:96
  105.7 5.9 broadcast_select_fusion.1
  114.6 3.1 copy.55
  117.8 4.5 fusion.57
  122.3 4.4 fusion.5
  126.7 8.0 %copy.53 = bf16[32,512,128]{1,0,2:T(8,128)(2,1)} copy(bf16[32,512,128]{2,1,0:T(8,128)(2,1)} %fusion.5) | data formatting | bytes 8388608 | tf_op jit(solution)/shard_map/convert_element_type | solution.py:46
  134.7 140.6 %all-reduce.6.cloned.1.call-done = (bf16[32,512,128]{2,1,0:T(8,128)(2,1)}, bf16[32,512,128]{2,1,0:T(8,128)(2,1)}) async-done(((bf16[32,512,128]{2,1,0:T(8,128)(2,1)}, bf16[32,512,128]{2,1,0:T(8,128)(2,1)}), (bf16[32,512,128]{2,1,0:T(8,128)(2,1)}, bf16[32,512,128]{2,1,0:T(8,128)(2,1)})) %all-reduce.6.cloned.1.call-update) | async-done | bytes 8388624 | tf_op jit(solution)/shard_map/psum | solution.py:11
  275.3 19.0 %fusion.10 = f32[64,512,256]{2,1,0:T(8,128)} fusion(bf16[32,512,128]{2,1,0:T(8,128)(2,1)} %get-tuple-element.14, bf16[32,512,128]{2,1,0:T(8,128)(2,1)} %get-tuple-element.15, bf16[128,256]{1,0:T(8,128)(2,1)S(1)} %copy-done), kind=kOutput, calls=%fused_computation.14 | convolution fusion | flops 2151677952 | bytes 42008576 | tf_op jit(solution)/shard_map/ikc,ch->ikh/dot_general | solution.py:42
  294.3 16.2 %fusion = bf16[64,512,128]{2,1,0:T(8,128)(2,1)} fusion(f32[64,512,256]{2,1,0:T(8,128)} %fusion.10, f32[64,512]{1,0:T(8,128)S(1)} %and_convert_fusion), kind=kLoop, calls=%fused_computation.1 | loop fusion | flops 25165824 | bytes 42074112 | tf_op jit(solution)/shard_map/convert_element_type | solution.py:46
  310.6 12.5 %copy.52 = bf16[64,512,128]{1,0,2:T(8,128)(2,1)} copy(bf16[64,512,128]{2,1,0:T(8,128)(2,1)} %fusion) | data formatting | bytes 16777216 | tf_op jit(solution)/shard_map/convert_element_type | solution.py:46
  323.1 6.9 bitcast_reduce_fusion
  334.5 5.6 convert_bitcast_fusion
  340.1 13.0 %copy.60 = bf16[64,512,128]{2,1,0:T(8,128)(2,1)} copy(bf16[64,512,128]{1,0,2:T(8,128)(2,1)} %convert_bitcast_fusion) | data formatting | bytes 16777216 | tf_op jit(solution)/shard_map/convert_element_type | solution.py:138
  353.1 102.8 %reduce-scatter.2.cloned.1.call-done = bf16[4,512,128]{2,1,0:T(8,128)(2,1)} async-done(((bf16[64,512,128]{2,1,0:T(8,128)(2,1)}), bf16[4,512,128]{2,1,0:T(8,128)(2,1)}) %reduce-scatter.2.cloned.1.call-update) | async-done | bytes 524304 | tf_op jit(solution)/shard_map/reduce_scatter | solution.py:137
  458.2 4.1 all-to-all-start.1
  462.2 6.6 convert_bitcast_fusion.1
  468.9 7.9 %copy.57 = bf16[32,512,128]{2,1,0:T(8,128)(2,1)} copy(bf16[32,512,128]{1,0,2:T(8,128)(2,1)} %convert_bitcast_fusion.1) | data formatting | bytes 8388608 | tf_op jit(solution)/shard_map/convert_element_type | solution.py:136
  476.7 5.5 copy.58
  482.2 5.3 all-to-all-start
  492.6 53.0 %all-to-all-done = bf16[8,32,64,128]{3,2,1,0:T(8,128)(2,1)} async-done(((bf16[8,32,64,128]{3,2,1,0:T(8,128)(2,1)}), bf16[8,32,64,128]{3,2,1,0:T(8,128)(2,1)}, u32[]{:S(2)}, u32[]{:S(2)}) %all-to-all-start) | async-done | bytes 4194336 | tf_op jit(solution)/shard_map/all_to_all | solution.py:22
  545.6 7.4 %all-to-all-start.2 = ((bf16[16,4,64,128]{3,2,1,0:T(8,128)(2,1)}), bf16[16,4,64,128]{3,2,1,0:T(8,128)(2,1)}, u32[]{:S(2)}, u32[]{:S(2)}) async-start(bf16[16,4,64,128]{3,2,1,0:T(8,128)(2,1)} %bitcast_multiply_fusion), calls=%async_computation.3 | async-start | bytes 2097152 | tf_op jit(solution)/shard_map/all_to_all | solution.py:146
  558.8 4.1 convert_reduce_fusion
  563.0 7.4 %all-to-all-done.2 = bf16[16,4,64,128]{3,2,1,0:T(8,128)(2,1)} async-done(((bf16[16,4,64,128]{3,2,1,0:T(8,128)(2,1)}), bf16[16,4,64,128]{3,2,1,0:T(8,128)(2,1)}, u32[]{:S(2)}, u32[]{:S(2)}) %all-to-all-start.2) | async-done | bytes 1048608 | tf_op jit(solution)/shard_map/all_to_all | solution.py:146
  582.9 136.8 %all-reduce.4.cloned.1.call-done = f32[98816]{0:T(1024)} async-done(((f32[98816]{0:T(1024)}), f32[98816]{0:T(1024)}) %all-reduce.4.cloned.1.call-update) | async-done | bytes 395280 | tf_op jit(solution)/shard_map/psum | solution.py:28
  (96 shorter events, 43.2 us)
Async XLA Ops:
  7.2 268.1 %copy-start = (bf16[128,256]{1,0:T(8,128)(2,1)S(1)}, bf16[128,256]{1,0:T(8,128)(2,1)}, u32[]{:S(2)}) copy-start(bf16[128,256]{1,0:T(8,128)(2,1)} %param.17) | copy-start | bytes 196612
  7.2 98.6 %all-gather.2.cloned.1.call-start = ((), (), s32[]{:S(2)}) async-start(), calls=%async_computation.4 | async-start | bytes 4718592 | tf_op jit(solution)/shard_map/all_gather | solution.py:96
  12.8 262.5 %all-reduce.6.cloned.1.call-start = ((), (), s32[]{:S(2)}) async-start(), calls=%async_computation.7 | async-start | bytes 16777216 | tf_op jit(solution)/shard_map/psum | solution.py:11
  111.7 1.0 copy-start.5
  111.7 1.0 copy-start.14
  111.7 1.4 copy-start.7
  111.7 1.4 copy-start.13
  111.7 344.2 %reduce-scatter.2.cloned.1.call-start = ((), (), s32[]{:S(2)}) async-start(), calls=%async_computation.5 | async-start | bytes 8912896 | tf_op jit(solution)/shard_map/reduce_scatter | solution.py:137
  112.7 5.1 copy-start.12
  323.1 7.3 copy-start.16
  330.0 1.7 copy-start.17
  331.6 2.9 copy-start.1
  333.5 1.0 copy-start.2
  353.1 109.2 %copy-start.3 = (bf16[32,64,128]{1,0,2:T(8,128)(2,1)S(1)}, bf16[32,64,128]{1,0,2:T(8,128)(2,1)}, u32[]{:S(2)}) copy-start(bf16[32,64,128]{1,0,2:T(8,128)(2,1)} %copy-done.2) | copy-start | bytes 1572868
  458.2 24.1 %all-to-all-start.1 = ((bf16[1,4,512,128]{3,1,0,2:T(4,128)(2,1)}), bf16[1,4,512,128]{3,1,0,2:T(4,128)(2,1)S(1)}, u32[]{:S(2)}, u32[]{:S(2)}) async-start(bf16[1,4,512,128]{3,1,0,2:T(4,128)(2,1)} %copy.61), calls=%async_computation.2 | async-start | bytes 1048576 | tf_op jit(solution)/shard_map/all_to_all | solution.py:141
  482.2 5.4 copy-start.6
  482.2 63.3 %all-to-all-start = ((bf16[8,32,64,128]{3,2,1,0:T(8,128)(2,1)}), bf16[8,32,64,128]{3,2,1,0:T(8,128)(2,1)}, u32[]{:S(2)}, u32[]{:S(2)}) async-start(bf16[8,32,64,128]{3,2,1,0:T(8,128)(2,1)} %copy.58), calls=%async_computation | async-start | bytes 8388608 | tf_op jit(solution)/shard_map/all_to_all | solution.py:22
  489.4 66.2 %copy-start.8 = (bf16[32,64,128]{2,1,0:T(8,128)(2,1)S(1)}, bf16[32,64,128]{2,1,0:T(8,128)(2,1)}, u32[]{:S(2)}) copy-start(bf16[32,64,128]{2,1,0:T(8,128)(2,1)} %param.12) | copy-start | bytes 1572868
  545.6 24.7 %all-to-all-start.2 = ((bf16[16,4,64,128]{3,2,1,0:T(8,128)(2,1)}), bf16[16,4,64,128]{3,2,1,0:T(8,128)(2,1)}, u32[]{:S(2)}, u32[]{:S(2)}) async-start(bf16[16,4,64,128]{3,2,1,0:T(8,128)(2,1)} %bitcast_multiply_fusion), calls=%async_computation.3 | async-start | bytes 2097152 | tf_op jit(solution)/shard_map/all_to_all | solution.py:146
  553.0 166.8 %all-reduce.4.cloned.1.call-start = ((), (), s32[]{:S(2)}) async-start(), calls=%async_computation.6 | async-start | bytes 794624 | tf_op jit(solution)/shard_map/psum | solution.py:28
  574.4 2.2 copy-start.11
  574.5 4.2 copy-start.9
  574.9 4.2 copy-start.4
  574.9 4.2 copy-start.15
  (1 other events, 0.8 us)
Sparse Core Ops, SparseCore 0:
  12.9 92.7 all-gather.1
  111.8 163.4 all-reduce.5
  353.2 102.6 reduce-scatter.1
  581.0 138.6 all-reduce.3
where the time goes:
time: 733 us; the launch traced here: 731 us
  waiting for transfers between devices  533 us (73%)
  local copies, waits for them, and re-layouts  60.6 us (8%)
  matrix products  54.7 us (7%)
  other arithmetic  50.7 us (7%)
  starting transfers between devices  17.1 us (2%)
  between operations  14.8 us (2%)
    psum x1, waiting for transfers between devices, broadcast(): return lax.psum(block, axis)  141 us
    psum x1, waiting for transfers between devices, together(): total = lax.psum(flat, axis)  137 us
    reduce_scatter x1, waiting for transfers between devices, per_device(): lax.psum_scatter(col_partial.astype(jnp.bfloat16), 'row', scatter_dimensi...  103 us
    all_gather x1, waiting for transfers between devices, per_device(): row_panel = lax.all_gather(normed, 'col', axis=1, tiled=True)  92.9 us
    all_to_all x1, waiting for transfers between devices, summed_on_arrival(): tiles = lax.all_to_all(split_up(x, dim, peers), axis, 0, 0, tiled=True)  53 us
    dot_general x4, matrix products, gating(): jnp.einsum('ikc,ch->ikh', panel, weight, preferred_element_type=jnp.float32)  27.1 us
    convert_element_type x2, other arithmetic, gating(): (pad_mask * sigmoid_val * values).astype(jnp.bfloat16)  20.6 us
    convert_element_type x2, local copies, waits for them, and re-layouts, gating(): (pad_mask * sigmoid_val * values).astype(jnp.bfloat16)  20.5 us
  transfers between devices with their start and end apart: 7, of which 6 were waited for; matrix products, arithmetic and copies ran while one was open for 8% of the time, Pallas kernels for 0%

commit v1 on v0

--- a/solution.py
+++ b/solution.py
@@ -93,7 +93,9 @@
     right_tile, right_val, right_sig, unused_mask = gating(
         normed, right_weight, own_ok, partner_ok, hidden
     )
-    row_panel = lax.all_gather(normed, "col", axis=1, tiled=True)
+    row_panel = jnp.concatenate(
+        lax.all_to_all(jnp.stack([normed] * lax.axis_size("col")), "col", 0, 0), axis=1
+    )
     pieces = []
     for member in range(per_col):
         pieces.append(broadcast(row_panel, "row", col_index * per_col + member))

time: 733 us -> 710 us (0.969)
  waiting for transfers between devices: 533 us -> 500 us
    all_gather x1 -> x0, waiting for transfers between devices: 92.9 us -> none  [per_device(): row_panel = lax.all_gather(normed, 'col', axis=1, tiled=True)]
    all_to_all x0 -> x1, waiting for transfers between devices: none -> 58.9 us  [per_device(): lax.all_to_all(jnp.stack([normed] * lax.axis_size('col')), 'col', 0, 0)]
where the time goes in v1:
time: 710 us; the launch traced here: 708 us
  waiting for transfers between devices  500 us (70%)
  local copies, waits for them, and re-layouts  66.6 us (9%)
  matrix products  54.7 us (8%)
  other arithmetic  48.4 us (7%)
  starting transfers between devices  23.6 us (3%)
  between operations  14.8 us (2%)
    psum x1, waiting for transfers between devices, broadcast(): return lax.psum(block, axis)  141 us
    psum x1, waiting for transfers between devices, together(): total = lax.psum(flat, axis)  137 us
    reduce_scatter x1, waiting for transfers between devices, per_device(): lax.psum_scatter(col_partial.astype(jnp.bfloat16), 'row', scatter_dimensi...  103 us
    all_to_all x1, waiting for transfers between devices, per_device(): lax.all_to_all(jnp.stack([normed] * lax.axis_size('col')), 'col', 0, 0)  58.9 us
    all_to_all x1, waiting for transfers between devices, summed_on_arrival(): tiles = lax.all_to_all(split_up(x, dim, peers), axis, 0, 0, tiled=True)  53 us
    dot_general x4, matrix products, gating(): jnp.einsum('ikc,ch->ikh', panel, weight, preferred_element_type=jnp.float32)  27.1 us
    convert_element_type x2, other arithmetic, gating(): (pad_mask * sigmoid_val * values).astype(jnp.bfloat16)  20.6 us
    convert_element_type x2, local copies, waits for them, and re-layouts, gating(): (pad_mask * sigmoid_val * values).astype(jnp.bfloat16)  20.5 us
  transfers between devices with their start and end apart: 7, of which 6 were waited for; matrix products, arithmetic and copies ran while one was open for 8% of the time, Pallas kernels for 0%

profile of v1, /device:TPU:1, one launch (start us, length us, event | category | flops | bytes accessed | tf_op | source)
XLA Modules:
  0.0 707.9 jit_solution(12645153200186953904)
XLA Ops:
  15.0 6.4 all-to-all-start
  21.5 58.9 %all-to-all-done = bf16[8,32,64,128]{3,2,1,0:T(8,128)(2,1)} async-done(((bf16[8,32,64,128]{3,2,1,0:T(8,128)(2,1)}), bf16[8,32,64,128]{3,2,1,0:T(8,128)(2,1)}, u32[]{:S(2)}, u32[]{:S(2)}) %all-to-all-start) | async-done | bytes 4194336 | tf_op jit(solution)/shard_map/all_to_all | solution.py:97
  83.6 4.4 broadcast_select_fusion.1
  94.1 4.5 fusion.57
  98.6 4.4 fusion.5
  103.0 8.0 %copy.55 = bf16[32,512,128]{1,0,2:T(8,128)(2,1)} copy(bf16[32,512,128]{2,1,0:T(8,128)(2,1)} %fusion.5) | data formatting | bytes 8388608 | tf_op jit(solution)/shard_map/convert_element_type | solution.py:46
  111.0 141.0 %all-reduce.6.cloned.1.call-done = (bf16[32,512,128]{2,1,0:T(8,128)(2,1)}, bf16[32,512,128]{2,1,0:T(8,128)(2,1)}) async-done(((bf16[32,512,128]{2,1,0:T(8,128)(2,1)}, bf16[32,512,128]{2,1,0:T(8,128)(2,1)}), (bf16[32,512,128]{2,1,0:T(8,128)(2,1)}, bf16[32,512,128]{2,1,0:T(8,128)(2,1)})) %all-reduce.6.cloned.1.call-update) | async-done | bytes 8388624 | tf_op jit(solution)/shard_map/psum | solution.py:11
  252.0 19.0 %fusion.10 = f32[64,512,256]{2,1,0:T(8,128)} fusion(bf16[32,512,128]{2,1,0:T(8,128)(2,1)} %get-tuple-element.14, bf16[32,512,128]{2,1,0:T(8,128)(2,1)} %get-tuple-element.15, bf16[128,256]{1,0:T(8,128)(2,1)S(1)} %copy-done), kind=kOutput, calls=%fused_computation.14 | convolution fusion | flops 2151677952 | bytes 42008576 | tf_op jit(solution)/shard_map/ikc,ch->ikh/dot_general | solution.py:42
  271.0 16.2 %fusion = bf16[64,512,128]{2,1,0:T(8,128)(2,1)} fusion(f32[64,512,256]{2,1,0:T(8,128)} %fusion.10, f32[64,512]{1,0:T(8,128)S(1)} %and_convert_fusion), kind=kLoop, calls=%fused_computation.1 | loop fusion | flops 25165824 | bytes 42074112 | tf_op jit(solution)/shard_map/convert_element_type | solution.py:46
  287.2 12.5 %copy.54 = bf16[64,512,128]{1,0,2:T(8,128)(2,1)} copy(bf16[64,512,128]{2,1,0:T(8,128)(2,1)} %fusion) | data formatting | bytes 16777216 | tf_op jit(solution)/shard_map/convert_element_type | solution.py:46
  299.8 6.9 bitcast_reduce_fusion
  311.2 5.6 convert_bitcast_fusion
  316.8 13.0 %copy.62 = bf16[64,512,128]{2,1,0:T(8,128)(2,1)} copy(bf16[64,512,128]{1,0,2:T(8,128)(2,1)} %convert_bitcast_fusion) | data formatting | bytes 16777216 | tf_op jit(solution)/shard_map/convert_element_type | solution.py:140
  329.8 102.8 %reduce-scatter.2.cloned.1.call-done = bf16[4,512,128]{2,1,0:T(8,128)(2,1)} async-done(((bf16[64,512,128]{2,1,0:T(8,128)(2,1)}), bf16[4,512,128]{2,1,0:T(8,128)(2,1)}) %reduce-scatter.2.cloned.1.call-update) | async-done | bytes 524304 | tf_op jit(solution)/shard_map/reduce_scatter | solution.py:139
  434.8 4.1 all-to-all-start.2
  438.9 6.6 convert_bitcast_fusion.1
  445.5 7.9 %copy.59 = bf16[32,512,128]{2,1,0:T(8,128)(2,1)} copy(bf16[32,512,128]{1,0,2:T(8,128)(2,1)} %convert_bitcast_fusion.1) | data formatting | bytes 8388608 | tf_op jit(solution)/shard_map/convert_element_type | solution.py:138
  453.4 5.5 copy.60
  458.9 5.3 all-to-all-start.1
  469.2 53.0 %all-to-all-done.1 = bf16[8,32,64,128]{3,2,1,0:T(8,128)(2,1)} async-done(((bf16[8,32,64,128]{3,2,1,0:T(8,128)(2,1)}), bf16[8,32,64,128]{3,2,1,0:T(8,128)(2,1)}, u32[]{:S(2)}, u32[]{:S(2)}) %all-to-all-start.1) | async-done | bytes 4194336 | tf_op jit(solution)/shard_map/all_to_all | solution.py:22
  522.2 7.4 %all-to-all-start.3 = ((bf16[16,4,64,128]{3,2,1,0:T(8,128)(2,1)}), bf16[16,4,64,128]{3,2,1,0:T(8,128)(2,1)}, u32[]{:S(2)}, u32[]{:S(2)}) async-start(bf16[16,4,64,128]{3,2,1,0:T(8,128)(2,1)} %bitcast_multiply_fusion), calls=%async_computation.4 | async-start | bytes 2097152 | tf_op jit(solution)/shard_map/all_to_all | solution.py:148
  535.5 4.1 convert_reduce_fusion
  539.7 7.3 %all-to-all-done.3 = bf16[16,4,64,128]{3,2,1,0:T(8,128)(2,1)} async-done(((bf16[16,4,64,128]{3,2,1,0:T(8,128)(2,1)}), bf16[16,4,64,128]{3,2,1,0:T(8,128)(2,1)}, u32[]{:S(2)}, u32[]{:S(2)}) %all-to-all-start.3) | async-done | bytes 1048608 | tf_op jit(solution)/shard_map/all_to_all | solution.py:148
  559.5 136.7 %all-reduce.4.cloned.1.call-done = f32[98816]{0:T(1024)} async-done(((f32[98816]{0:T(1024)}), f32[98816]{0:T(1024)}) %all-reduce.4.cloned.1.call-update) | async-done | bytes 395280 | tf_op jit(solution)/shard_map/psum | solution.py:28
  (99 shorter events, 51.6 us)
Async XLA Ops:
  7.2 244.8 %copy-start = (bf16[128,256]{1,0:T(8,128)(2,1)S(1)}, bf16[128,256]{1,0:T(8,128)(2,1)}, u32[]{:S(2)}) copy-start(bf16[128,256]{1,0:T(8,128)(2,1)} %param.17) | copy-start | bytes 196612
  12.0 77.0 %copy-start.6 = (bf16[32,64,128]{2,1,0:T(8,128)(2,1)}, bf16[32,64,128]{2,1,0:T(8,128)(2,1)S(1)}, u32[]{:S(2)}) copy-start(bf16[32,64,128]{2,1,0:T(8,128)(2,1)S(1)} %fusion.27) | copy-start | bytes 1572868
  15.0 65.4 %all-to-all-start = ((bf16[8,32,64,128]{3,2,1,0:T(8,128)(2,1)}), bf16[8,32,64,128]{3,2,1,0:T(8,128)(2,1)}, u32[]{:S(2)}, u32[]{:S(2)}) async-start(bf16[8,32,64,128]{3,2,1,0:T(8,128)(2,1)} %stack.12), calls=%async_computation | async-start | bytes 8388608 | tf_op jit(solution)/shard_map/all_to_all | solution.py:97
  21.4 230.6 %all-reduce.6.cloned.1.call-start = ((), (), s32[]{:S(2)}) async-start(), calls=%async_computation.7 | async-start | bytes 16777216 | tf_op jit(solution)/shard_map/psum | solution.py:11
  83.5 4.5 copy-start.1
  88.1 1.4 copy-start.8
  88.1 1.4 copy-start.14
  88.1 344.5 %reduce-scatter.2.cloned.1.call-start = ((), (), s32[]{:S(2)}) async-start(), calls=%async_computation.5 | async-start | bytes 8912896 | tf_op jit(solution)/shard_map/reduce_scatter | solution.py:139
  89.0 5.1 copy-start.13
  299.8 7.3 %copy-start.17 = (f32[128]{0:T(128)S(1)}, f32[128]{0:T(128)}, u32[]{:S(2)}) copy-start(f32[128]{0:T(128)} %param.19) | copy-start | bytes 1540
  306.7 1.7 copy-start.18
  308.3 2.9 copy-start.2
  310.2 1.0 copy-start.3
  329.8 109.1 %copy-start.4 = (bf16[32,64,128]{1,0,2:T(8,128)(2,1)S(1)}, bf16[32,64,128]{1,0,2:T(8,128)(2,1)}, u32[]{:S(2)}) copy-start(bf16[32,64,128]{1,0,2:T(8,128)(2,1)} %copy-done.3) | copy-start | bytes 1572868
  434.8 24.1 %all-to-all-start.2 = ((bf16[1,4,512,128]{3,1,0,2:T(4,128)(2,1)}), bf16[1,4,512,128]{3,1,0,2:T(4,128)(2,1)S(1)}, u32[]{:S(2)}, u32[]{:S(2)}) async-start(bf16[1,4,512,128]{3,1,0,2:T(4,128)(2,1)} %copy.63), calls=%async_computation.3 | async-start | bytes 1048576 | tf_op jit(solution)/shard_map/all_to_all | solution.py:143
  458.9 5.4 copy-start.7
  458.9 63.3 %all-to-all-start.1 = ((bf16[8,32,64,128]{3,2,1,0:T(8,128)(2,1)}), bf16[8,32,64,128]{3,2,1,0:T(8,128)(2,1)}, u32[]{:S(2)}, u32[]{:S(2)}) async-start(bf16[8,32,64,128]{3,2,1,0:T(8,128)(2,1)} %copy.60), calls=%async_computation.1 | async-start | bytes 8388608 | tf_op jit(solution)/shard_map/all_to_all | solution.py:22
  466.0 66.2 %copy-start.9 = (bf16[32,64,128]{2,1,0:T(8,128)(2,1)S(1)}, bf16[32,64,128]{2,1,0:T(8,128)(2,1)}, u32[]{:S(2)}) copy-start(bf16[32,64,128]{2,1,0:T(8,128)(2,1)} %param.12) | copy-start | bytes 1572868
  522.2 24.8 %all-to-all-start.3 = ((bf16[16,4,64,128]{3,2,1,0:T(8,128)(2,1)}), bf16[16,4,64,128]{3,2,1,0:T(8,128)(2,1)}, u32[]{:S(2)}, u32[]{:S(2)}) async-start(bf16[16,4,64,128]{3,2,1,0:T(8,128)(2,1)} %bitcast_multiply_fusion), calls=%async_computation.4 | async-start | bytes 2097152 | tf_op jit(solution)/shard_map/all_to_all | solution.py:148
  529.6 166.7 %all-reduce.4.cloned.1.call-start = ((), (), s32[]{:S(2)}) async-start(), calls=%async_computation.6 | async-start | bytes 794624 | tf_op jit(solution)/shard_map/psum | solution.py:28
  551.1 2.2 copy-start.12
  551.1 4.2 copy-start.10
  551.5 4.2 copy-start.5
  551.6 4.2 copy-start.16
  (2 other events, 1.7 us)
Sparse Core Ops, SparseCore 0:
  88.2 163.7 all-reduce.5
  329.9 102.6 reduce-scatter.1
  557.7 138.5 all-reduce.3
